TPU v7x, 32 devices: a whole 2x2x4 slice. The times are simulated.
32 devices in a mesh: dp: 8 (over y, x, core), seq: 4 (over z).
Axes of the slice: x: 2, y: 2, z: 4, core: 2. Of those that a mesh axis runs over, the one named last changes fastest.
Arguments:
- hidden_in: bfloat16 [8, 512, 2048], P('dp', 'seq'), may hold values from -6 to 6
- cotangent: bfloat16 [8, 512, 2048], P('dp', 'seq'), may hold values from -6 to 6
- norm_gain: float32 [2048], P('dp'), may hold values from 0.1 to 1.9
- route_weights: float32 [8, 512, 10], P('dp', 'seq'), may hold values from 0.1 to 1
- expert_ids: int32 [8, 512, 10], P('dp', 'seq'), may hold values from 0 to 63, all different within a row; in each aligned block of 128 rows (0 to 127, 128 to 255, ..., all dimensions but the last counted through in order) at most 24 rows name the same one
- expert_gate: bfloat16 [64, 2048, 512], P(('dp', 'seq')), may hold values from -0.125 to 0.125
- expert_up: bfloat16 [64, 2048, 512], P(('dp', 'seq')), may hold values from -0.125 to 0.125
- expert_down: bfloat16 [64, 512, 2048], P(('dp', 'seq')), may hold values from -0.25 to 0.25
Outputs:
- grad_hidden: bfloat16 [8, 512, 2048], P('dp', 'seq')
- grad_gain: float32 [2048], P('dp')
- grad_gate: bfloat16 [64, 2048, 512], P(('dp', 'seq'))
- grad_up: bfloat16 [64, 2048, 512], P(('dp', 'seq'))
- grad_down: bfloat16 [64, 512, 2048], P(('dp', 'seq'))
Inputs may be any that keep to these rules, and one draw needn't show every extreme that they name: `expert_ids`: each token names 10 different experts. Among the rows of one device no expert is named by more than 24 of them, and in some device one expert is named by exactly 24.
All inputs are finite; a program needn't handle non-finite values.
Results may differ from a plain program's by a relative error of at most 0.0072.
Values may be sent and summed in bfloat16 or wider, within the bound.
A program may use at most 192 MiB of HBM per device.

v0:
```python
import jax
import jax.numpy as jnp
from jax import lax
from jax.sharding import PartitionSpec as P

TOP = 10


EPSILON = 1e-06


def shards(
    hidden_in, cotangent, norm_gain, route_weights, expert_ids, expert_gate, expert_up, expert_down
):
    tokens_here = hidden_in.shape[1]
    model_width = hidden_in.shape[2]
    local_experts = expert_gate.shape[0]
    dp_count = lax.axis_size("dp")
    seq_count = lax.axis_size("seq")
    devices = dp_count * seq_count
    expert_count = local_experts * devices
    capacity = max(2, tokens_here * TOP * 6 // (5 * expert_count))
    assignments = tokens_here * TOP
    gain_full = lax.all_gather(norm_gain, "dp", axis=0, tiled=True)
    inputs = hidden_in[0].astype(jnp.float32)
    inverse_root = lax.rsqrt(jnp.mean(inputs * inputs, axis=1, keepdims=True) + EPSILON)
    scaled = inputs * inverse_root
    normed = (scaled * gain_full[None, :]).astype(jnp.bfloat16)
    upstream = cotangent[0]
    weighted = (route_weights[0][:, :, None] * upstream[:, None, :].astype(jnp.float32)).astype(
        jnp.bfloat16
    )
    weighted = weighted.reshape(assignments, model_width)
    flat_experts = expert_ids[0].reshape(assignments)
    onehot = (flat_experts[:, None] == jnp.arange(expert_count, dtype=jnp.int32)[None, :]).astype(
        jnp.bfloat16
    )
    position = jnp.arange(assignments, dtype=jnp.int32)
    earlier = (position[:, None] > position[None, :]).astype(jnp.bfloat16)
    before = jnp.dot(earlier, onehot, preferred_element_type=jnp.float32)
    earlier_count = jnp.sum(before * onehot.astype(jnp.float32), axis=1).astype(jnp.int32)
    slot_index = flat_experts * capacity + earlier_count
    slot_entry = jnp.zeros((expert_count * capacity,), jnp.int32).at[slot_index].set(position + 1)
    occupied = slot_entry > 0
    source = jnp.maximum(slot_entry - 1, 0)
    zero_value = jnp.zeros((), jnp.bfloat16)
    flat_shape = (devices, local_experts * capacity, model_width)
    send_rows = jnp.where(occupied[:, None], normed[source // TOP], zero_value).reshape(flat_shape)
    send_grads = jnp.where(occupied[:, None], weighted[source], zero_value).reshape(flat_shape)
    arrived_rows, arrived_grads = (
        lax.all_to_all(send_rows, ("dp", "seq"), split_axis=0, concat_axis=0, tiled=True),
        lax.all_to_all(send_grads, ("dp", "seq"), split_axis=0, concat_axis=0, tiled=True),
    )
    four_shape = (devices, local_experts, capacity, model_width)
    rows_in = arrived_rows.reshape(four_shape)
    rows_grad = arrived_grads.reshape(four_shape)
    pre_gate = jnp.einsum(
        "nicd,idf->nicf", rows_in, expert_gate, preferred_element_type=jnp.float32
    )
    pre_up = jnp.einsum("nicd,idf->nicf", rows_in, expert_up, preferred_element_type=jnp.float32)
    sigmoid_gate = jax.nn.sigmoid(pre_gate)
    silu_gate = pre_gate * sigmoid_gate
    activation = (silu_gate * pre_up).astype(jnp.bfloat16)
    grad_act = jnp.einsum(
        "nicd,ifd->nicf", rows_grad, expert_down, preferred_element_type=jnp.float32
    )
    gate_back = (grad_act * pre_up * sigmoid_gate * (1.0 + pre_gate * (1.0 - sigmoid_gate))).astype(
        jnp.bfloat16
    )
    up_back = (grad_act * silu_gate).astype(jnp.bfloat16)
    grad_down = jnp.einsum(
        "nicf,nicd->ifd", activation, rows_grad, preferred_element_type=jnp.float32
    ).astype(jnp.bfloat16)
    grad_gate = jnp.einsum(
        "nicd,nicf->idf", rows_in, gate_back, preferred_element_type=jnp.float32
    ).astype(jnp.bfloat16)
    grad_up = jnp.einsum(
        "nicd,nicf->idf", rows_in, up_back, preferred_element_type=jnp.float32
    ).astype(jnp.bfloat16)
    returned = (
        jnp.einsum("nicf,idf->nicd", gate_back, expert_gate, preferred_element_type=jnp.float32)
        + jnp.einsum("nicf,idf->nicd", up_back, expert_up, preferred_element_type=jnp.float32)
    ).astype(jnp.bfloat16)
    back_rows = lax.all_to_all(
        returned.reshape(flat_shape), ("dp", "seq"), split_axis=0, concat_axis=0, tiled=True
    )
    back_flat = back_rows.reshape(expert_count * capacity, model_width)
    summed = jnp.sum(
        back_flat[slot_index].astype(jnp.float32).reshape(tokens_here, TOP, model_width), axis=1
    )
    local_gain = jnp.sum(summed * scaled, axis=0)
    partial_share = lax.psum_scatter(local_gain, "dp", scatter_dimension=0, tiled=True)
    grad_gain = lax.psum(partial_share, "seq")
    gained = summed * gain_full[None, :]
    centered = jnp.mean(gained * scaled, axis=1, keepdims=True)
    grad_hidden = (
        upstream.astype(jnp.float32) + inverse_root * (gained - scaled * centered)
    ).astype(jnp.bfloat16)
    return (grad_hidden.reshape(hidden_in.shape), grad_gain, grad_gate, grad_up, grad_down)


def solution(mesh):
    return jax.shard_map(
        shards,
        mesh=mesh,
        in_specs=(
            P("dp", "seq", None),
            P("dp", "seq", None),
            P("dp"),
            P("dp", "seq", None),
            P("dp", "seq", None),
            P(("dp", "seq"), None, None),
            P(("dp", "seq"), None, None),
            P(("dp", "seq"), None, None),
        ),
        out_specs=(
            P("dp", "seq", None),
            P("dp"),
            P(("dp", "seq"), None, None),
            P(("dp", "seq"), None, None),
            P(("dp", "seq"), None, None),
        ),
        check_vma=False,
    )
```

profile of v0, /device:TPU:0, one launch (start us, length us, event | category | flops | bytes accessed | tf_op | source)
XLA Modules:
  0.0 598.8 jit_solution(17626287329584033442)
XLA Ops:
  0.7 0.0 copy-start.4
  0.7 0.8 broadcast_multiply_fusion
  1.5 0.8 copy.33
  2.3 0.1 copy.32
  2.4 0.1 mul.125
  2.5 0.1 eq.15
  2.6 0.8 fusion.36
  3.5 5.2 scatter_custom_fusion
  8.8 0.2 fusion.41
  9.0 10.4 %all-gather = f32[8,1,256]{2,1,0:T(1,128)S(1)} all-gather(f32[1,1,256]{2,1,0:T(1,128)S(1)} %bitcast.124), channel_id=1, replica_groups=mesh['dp'=8,'seq'=4] {'dp'}, dimensions={0}, use_global_device_ids=true | all-gather | bytes 9216 | tf_op jit(solution)/shard_map/all_gather | solution.py:24
  19.5 0.1 copy.34
  19.6 0.1 mul.127
  19.7 0.1 broadcast_in_dim.35
  19.8 0.1 convert_bitcast_fusion.1
  19.9 7.9 %mul.129 = f32[128,10,2048]{2,1,0:T(8,128)} broadcast(f32[128,2048]{1,0:T(8,128)S(1)} %convert_bitcast_fusion.1), dimensions={0,2} | broadcast | bytes 11534336 | tf_op jit(solution)/shard_map/mul | solution.py:30
  27.9 13.9 %mul.130 = f32[1280,2048]{1,0:T(8,128)} reshape(f32[128,10,2048]{2,1,0:T(8,128)} %mul.129) | data formatting | bytes 20971520 | tf_op jit(solution)/shard_map/mul | solution.py:30
  41.8 0.2 fusion.38
  42.0 7.1 %gather_fusion.1 = bf16[1536,2048]{1,0:T(8,128)(2,1)} fusion(bf16[128,2048]{1,0:T(8,128)(2,1)S(1)} %fusion.38, s32[2048]{0:T(1024)S(1)} %pad_clamp_fusion.1), kind=kCustom, calls=%fused_computation.1 | custom fusion | bytes 12589056 | tf_op jit(solution)/shard_map/gather | solution.py:48
  49.1 7.0 %multiply_convert_fusion = bf16[1280,2048]{1,0:T(8,128)(2,1)} fusion(f32[1280,2048]{1,0:T(8,128)} %mul.130, f32[1280]{0:T(1024)S(1)} %mul.127), kind=kLoop, calls=%fused_computation.5 | loop fusion | flops 5242880 | bytes 15733760 | tf_op jit(solution)/shard_map/convert_element_type | solution.py:30
  56.1 15.9 %gather_fusion = bf16[1536,2048]{1,0:T(8,128)(2,1)} fusion(bf16[1280,2048]{1,0:T(8,128)(2,1)} %multiply_convert_fusion, s32[2048]{0:T(1024)S(1)} %pad_clamp_fusion.2), kind=kCustom, calls=%fused_computation | custom fusion | bytes 12589056 | tf_op jit(solution)/shard_map/gather | solution.py:49
  72.0 8.3 %broadcast_select_fusion.1 = (bf16[32,48,2048]{2,1,0:T(8,128)(2,1)}, bf16[32,48,2048]{2,1,0:T(8,128)(2,1)S(1)}) fusion(bf16[32,48,2048]{2,1,0:T(8,128)(2,1)} %bitcast.112, pred[32,48]{1,0:T(8,128)(4,1)S(1)} %broadcast_in_dim.35, bf16[32,48,2048]{2,1,0:T(8,128)(2,1)} %bitcast.111), kind=kLoop, calls=%fused_computation.13 | loop fusion | flops 6291456 | bytes 25167360 | tf_op jit(solution)/shard_map/jit(_where)/select_n | solution.py:49
  80.2 142.1 %all_to_all.15 = bf16[32,48,2048]{2,1,0:T(8,128)(2,1)} all-to-all(bf16[32,48,2048]{2,1,0:T(8,128)(2,1)S(1)} %get-tuple-element.12), channel_id=1, replica_groups=mesh['dp'=8,'seq'=4] {'dp','seq'}, dimensions={0} | all-to-all | bytes 12582912 | tf_op jit(solution)/shard_map/all_to_all | solution.py:51
  222.3 4.8 all-to-all-start
  227.2 9.3 %fusion.2 = f32[2,32,24,512]{3,2,1,0:T(8,128)} fusion(bf16[32,2,24,2048]{3,2,1,0:T(8,128)(2,1)} %bitcast.113, bf16[2,2048,512]{2,1,0:T(8,128)(2,1)} %param.13), kind=kOutput, calls=%fused_computation.14 | convolution fusion | flops 3221225472 | bytes 13631488 | tf_op jit(solution)/shard_map/nicd,idf->nicf/dot_general | solution.py:57
  236.4 5.2 fusion.4
  241.6 122.2 %all-to-all-done = bf16[32,48,2048]{2,1,0:T(8,128)(2,1)} async-done(((bf16[32,48,2048]{2,1,0:T(8,128)(2,1)}), bf16[32,48,2048]{2,1,0:T(8,128)(2,1)}, u32[]{:S(2)}, u32[]{:S(2)}) %all-to-all-start) | async-done | bytes 6291488 | tf_op jit(solution)/shard_map/all_to_all | solution.py:52
  363.8 10.4 %fusion.26 = (bf16[32,2,24,512]{3,2,0,1:T(8,128)(2,1)S(1)}, bf16[32,2,24,512]{3,2,0,1:T(8,128)(2,1)S(1)}) fusion(f32[2,32,24,512]{3,2,1,0:T(8,128)} %fusion.2, f32[2,32,24,512]{3,2,1,0:T(8,128)} %fusion.4, bf16[2,512,2048]{2,1,0:T(8,128)(2,1)} %param.15, bf16[32,2,24,2048]{3,2,1,0:T(8,128)(2,1)} %bitcast.3), kind=kOutput, calls=%fused_computation.42 | convolution fusion | flops 3231449088 | bytes 19922944 | tf_op jit(solution)/shard_map/nicd,ifd->nicf/dot_general | solution.py:64
  374.2 6.4 %fusion.10 = f32[2,32,24,2048]{3,2,1,0:T(8,128)} fusion(bf16[32,2,24,512]{3,2,0,1:T(8,128)(2,1)S(1)} %get-tuple-element.8, bf16[2,2048,512]{2,1,0:T(8,128)(2,1)S(1)} %copy-done.2), kind=kOutput, calls=%fused_computation.22 | convolution fusion | flops 3221225472 | bytes 18350080 | tf_op jit(solution)/shard_map/nicf,idf->nicd/dot_general | solution.py:81
  380.6 8.0 %fusion.1 = bf16[32,2,24,2048]{3,2,0,1:T(8,128)(2,1)S(1)} fusion(f32[2,32,24,2048]{3,2,1,0:T(8,128)} %fusion.10, bf16[32,2,24,512]{3,2,0,1:T(8,128)(2,1)S(1)} %get-tuple-element.7, bf16[2,2048,512]{2,1,0:T(8,128)(2,1)} %param.14), kind=kOutput, calls=%fused_computation.11 | convolution fusion | flops 3227516928 | bytes 24641536 | tf_op jit(solution)/shard_map/nicf,idf->nicd/dot_general | solution.py:82
  388.6 3.2 copy.38
  391.8 7.1 %all-to-all-start.2 = ((bf16[32,48,2048]{2,1,0:T(8,128)(2,1)}), bf16[32,48,2048]{2,1,0:T(8,128)(2,1)}, u32[]{:S(2)}, u32[]{:S(2)}) async-start(bf16[32,48,2048]{2,1,0:T(8,128)(2,1)} %bitcast.110), calls=%async_computation.2 | async-start | bytes 12582912 | tf_op jit(solution)/shard_map/all_to_all | solution.py:84
  398.9 0.6 dynamic-slice
  400.2 0.0 copy-start.7
  400.2 8.9 %bitcast_convert_fusion.1 = bf16[2,2048,512]{2,1,0:T(8,128)(2,1)} fusion(bf16[32,2,24,2048]{3,2,1,0:T(8,128)(2,1)} %bitcast.114, bf16[32,2,24,512]{3,2,0,1:T(8,128)(2,1)} %copy-done.8), kind=kOutput, calls=%fused_computation.7 | convolution fusion | flops 3223322624 | bytes 12058624 | tf_op jit(solution)/shard_map/nicd,nicf->idf/dot_general | solution.py:77
  409.1 0.0 copy-start.16
  409.1 5.1 bitcast_convert_fusion.2
  414.2 8.1 %bitcast_convert_fusion = bf16[2,512,2048]{2,1,0:T(8,128)(2,1)} fusion(bf16[32,2,24,2048]{3,2,1,0:T(8,128)(2,1)} %bitcast.3, f32[2,32,24,512]{3,2,1,0:T(8,128)S(1)} %copy-done.17, f32[2,32,24,512]{3,2,1,0:T(8,128)S(1)} %copy-done.16), kind=kOutput, calls=%fused_computation.6 | convolution fusion | flops 3228041216 | bytes 16777216 | tf_op jit(solution)/shard_map/nicf,nicd->ifd/dot_general | solution.py:71
  422.3 113.4 %all-to-all-done.2 = bf16[32,48,2048]{2,1,0:T(8,128)(2,1)} async-done(((bf16[32,48,2048]{2,1,0:T(8,128)(2,1)}), bf16[32,48,2048]{2,1,0:T(8,128)(2,1)}, u32[]{:S(2)}, u32[]{:S(2)}) %all-to-all-start.2) | async-done | bytes 6291488 | tf_op jit(solution)/shard_map/all_to_all | solution.py:84
  535.6 14.4 %gather_fusion.2 = bf16[1280,2048]{1,0:T(8,128)(2,1)} fusion(bf16[1536,2048]{1,0:T(8,128)(2,1)} %bitcast.20, s32[2048]{0:T(1024)S(1)} %pad_clamp_fusion), kind=kCustom, calls=%fused_computation.2 | custom fusion | bytes 10490880 | tf_op jit(solution)/shard_map/gather | solution.py:89
  550.0 10.6 %reshape.157 = f32[128,10,2048]{2,1,0:T(8,128)} reshape(bf16[1280,2048]{1,0:T(8,128)(2,1)} %gather_fusion.2) | data formatting | bytes 15728640 | tf_op jit(solution)/shard_map/convert_element_type | solution.py:89
  560.6 0.0 copy-start.10
  560.6 0.0 copy-start.13
  560.7 9.9 %reduce_sum.49 = f32[128,2048]{1,0:T(8,128)S(1)} reduce(f32[128,10,2048]{2,1,0:T(8,128)} %reshape.157, f32[]{:T(128)} %constant.12.clone.1), dimensions={1}, to_apply=%region_3.4 | reduce | flops 2359296 | bytes 11534340 | tf_op jit(solution)/shard_map/reduce_sum | solution.py:88
  570.6 0.4 fusion.40
  570.9 15.0 %all-reduce = f32[2048]{0:T(1024)S(1)} all-reduce(f32[2048]{0:T(1024)S(1)} %get-tuple-element.5), channel_id=2, replica_groups=mesh['dp'=8,'seq'=4] {'dp'}, use_global_device_ids=true, to_apply=%region_6.7.clone | all-reduce | flops 2048 | bytes 16384
  585.9 0.1 dynamic-slice.1
  586.0 11.1 %psum.7 = f32[256]{0:T(256)} all-reduce(f32[256]{0:T(256)S(1)} %dynamic-slice.1), channel_id=1, replica_groups=mesh['dp'=8,'seq'=4] {'seq'}, use_global_device_ids=true, to_apply=%region_7.8 | all-reduce | flops 256 | bytes 2048 | tf_op jit(solution)/shard_map/psum | solution.py:93
  597.1 1.2 fusion.37
  (51 shorter events, 0.2 us)
Async XLA Ops:
  0.6 8.2 %copy-start = (bf16[1,128,2048]{2,1,0:T(8,128)(2,1)S(1)}, bf16[1,128,2048]{2,1,0:T(8,128)(2,1)}, u32[]{:S(2)}) copy-start(bf16[1,128,2048]{2,1,0:T(8,128)(2,1)} %param.8) | copy-start | bytes 1572868
  0.6 8.4 %copy-start.14 = (f32[256]{0:T(256)S(1)}, f32[256]{0:T(256)}, u32[]{:S(2)}) copy-start(f32[256]{0:T(256)} %param.10) | copy-start | bytes 3076
  0.7 18.8 %copy-start.11 = (f32[1,128,10]{1,0,2:T(1,128)S(1)}, f32[1,128,10]{1,0,2:T(1,128)}, u32[]{:S(2)}) copy-start(f32[1,128,10]{1,0,2:T(1,128)} %param.11) | copy-start | bytes 15364
  0.7 19.2 %copy-start.4 = (bf16[1,128,2048]{2,1,0:T(8,128)(2,1)S(1)}, bf16[1,128,2048]{2,1,0:T(8,128)(2,1)}, u32[]{:S(2)}) copy-start(bf16[1,128,2048]{2,1,0:T(8,128)(2,1)} %param.9) | copy-start | bytes 1572868
  9.0 32.8 %copy-start.12 = (f32[128]{0:T(128)}, f32[128]{0:T(128)S(1)}, u32[]{:S(2)}) copy-start(f32[128]{0:T(128)S(1)} %add_rsqrt_fusion) | copy-start | bytes 1540
  19.5 22.3 %copy-start.9 = (f32[8,1,256]{2,1,0:T(1,128)}, f32[8,1,256]{2,1,0:T(1,128)S(1)}, u32[]{:S(2)}) copy-start(f32[8,1,256]{2,1,0:T(1,128)S(1)} %all-gather) | copy-start | bytes 24580
  222.3 14.1 %slice-start = ((s8[6291456]{0:T(1024)(128)(4,1)}), s8[2097152]{0:T(1024)(128)(4,1)S(1)}, s32[]{:S(2)}) async-start(s8[6291456]{0:T(1024)(128)(4,1)} %bitcast.115), calls=%async_computation.3 | async-start | bytes 4194304
  222.3 141.5 %all-to-all-start = ((bf16[32,48,2048]{2,1,0:T(8,128)(2,1)}), bf16[32,48,2048]{2,1,0:T(8,128)(2,1)}, u32[]{:S(2)}, u32[]{:S(2)}) async-start(bf16[32,48,2048]{2,1,0:T(8,128)(2,1)} %get-tuple-element.11), calls=%async_computation | async-start | bytes 12582912 | tf_op jit(solution)/shard_map/all_to_all | solution.py:52
  227.1 9.3 %slice-start.1 = ((s8[6291456]{0:T(1024)(128)(4,1)}), s8[4194304]{0:T(1024)(128)(4,1)S(1)}, s32[]{:S(2)}) async-start(s8[6291456]{0:T(1024)(128)(4,1)} %bitcast.115), calls=%async_computation.4 | async-start | bytes 8388608
  227.1 9.3 %copy-start.3 = (bf16[2,2048,512]{2,1,0:T(8,128)(2,1)S(1)}, bf16[2,2048,512]{2,1,0:T(8,128)(2,1)}, u32[]{:S(2)}) copy-start(bf16[2,2048,512]{2,1,0:T(8,128)(2,1)} %param.14) | copy-start | bytes 12582916
  363.8 10.4 %copy-start.2 = (bf16[2,2048,512]{2,1,0:T(8,128)(2,1)S(1)}, bf16[2,2048,512]{2,1,0:T(8,128)(2,1)}, u32[]{:S(2)}) copy-start(bf16[2,2048,512]{2,1,0:T(8,128)(2,1)} %param.13) | copy-start | bytes 12582916
  374.2 6.4 %copy-start.6 = (bf16[32,2,24,512]{3,2,0,1:T(8,128)(2,1)}, bf16[32,2,24,512]{3,2,0,1:T(8,128)(2,1)S(1)}, u32[]{:S(2)}) copy-start(bf16[32,2,24,512]{3,2,0,1:T(8,128)(2,1)S(1)} %get-tuple-element.8) | copy-start | bytes 4718596
  374.2 6.4 %copy-start.8 = (bf16[32,2,24,512]{3,2,0,1:T(8,128)(2,1)}, bf16[32,2,24,512]{3,2,0,1:T(8,128)(2,1)S(1)}, u32[]{:S(2)}) copy-start(bf16[32,2,24,512]{3,2,0,1:T(8,128)(2,1)S(1)} %get-tuple-element.7) | copy-start | bytes 4718596
  391.8 7.1 %copy-start.15 = (u32[32]{0:T(128)S(1)}, u32[32]{0:T(128)}, u32[]{:S(2)}) copy-start(u32[32]{0:T(128)} %constant.45) | copy-start | bytes 388
  391.8 17.2 %slice-start.2 = ((s8[6291456]{0:T(1024)(128)(4,1)}), s8[2097152]{0:T(1024)(128)(4,1)S(1)}, s32[]{:S(2)}) async-start(s8[6291456]{0:T(1024)(128)(4,1)} %bitcast.118), calls=%async_computation.5 | async-start | bytes 4194304
  391.8 143.8 %all-to-all-start.2 = ((bf16[32,48,2048]{2,1,0:T(8,128)(2,1)}), bf16[32,48,2048]{2,1,0:T(8,128)(2,1)}, u32[]{:S(2)}, u32[]{:S(2)}) async-start(bf16[32,48,2048]{2,1,0:T(8,128)(2,1)} %bitcast.110), calls=%async_computation.2 | async-start | bytes 12582912 | tf_op jit(solution)/shard_map/all_to_all | solution.py:84
  400.2 8.9 %slice-start.3 = ((s8[6291456]{0:T(1024)(128)(4,1)}), s8[4194304]{0:T(1024)(128)(4,1)S(1)}, s32[]{:S(2)}) async-start(s8[6291456]{0:T(1024)(128)(4,1)} %bitcast.118), calls=%async_computation.6 | async-start | bytes 8388608
  400.2 8.9 %copy-start.7 = (bf16[32,2,24,512]{3,2,0,1:T(8,128)(2,1)S(1)}, bf16[32,2,24,512]{3,2,0,1:T(8,128)(2,1)}, u32[]{:S(2)}) copy-start(bf16[32,2,24,512]{3,2,0,1:T(8,128)(2,1)} %copy-done.6) | copy-start | bytes 4718596
  409.1 5.1 copy-start.16
  409.1 5.1 copy-start.17
  560.6 9.9 %copy-start.1 = (bf16[1,128,2048]{2,1,0:T(8,128)(2,1)S(1)}, bf16[1,128,2048]{2,1,0:T(8,128)(2,1)}, u32[]{:S(2)}) copy-start(bf16[1,128,2048]{2,1,0:T(8,128)(2,1)} %param.8) | copy-start | bytes 1572868
  560.6 9.9 %copy-start.10 = (f32[8,1,256]{2,1,0:T(1,128)S(1)}, f32[8,1,256]{2,1,0:T(1,128)}, u32[]{:S(2)}) copy-start(f32[8,1,256]{2,1,0:T(1,128)} %copy-done.9) | copy-start | bytes 24580
  560.6 9.9 %copy-start.13 = (f32[128]{0:T(128)S(1)}, f32[128]{0:T(128)}, u32[]{:S(2)}) copy-start(f32[128]{0:T(128)} %copy-done.12) | copy-start | bytes 1540
  560.6 36.5 %copy-start.5 = (bf16[1,128,2048]{2,1,0:T(8,128)(2,1)S(1)}, bf16[1,128,2048]{2,1,0:T(8,128)(2,1)}, u32[]{:S(2)}) copy-start(bf16[1,128,2048]{2,1,0:T(8,128)(2,1)} %param.9) | copy-start | bytes 1572868
where the time goes:
time: 606 us; the launch traced here: 599 us
  waiting for transfers between devices  236 us (39%)
  blocking collectives  179 us (30%)
  local copies, waits for them, and re-layouts  80.5 us (13%)
  matrix products  62 us (10%)
  other arithmetic  28 us (5%)
  starting transfers between devices  11.9 us (2%)
    all_to_all x1, blocking collectives, shards(): lax.all_to_all(send_rows, ('dp', 'seq'), split_axis=0, concat_axis=0, til...  142 us
    all_to_all x1, waiting for transfers between devices, shards(): lax.all_to_all(send_grads, ('dp', 'seq'), split_axis=0, concat_axis=0, ti...  122 us
    all_to_all x1, waiting for transfers between devices, shards(): lax.all_to_all(returned.reshape(flat_shape), ('dp', 'seq'), split_axis=0,...  113 us
    mul x3, local copies, waits for them, and re-layouts, shards(): route_weights[0][:, :, None] * upstream[:, None, :].astype(jnp.float32)  22 us
    gather x1, local copies, waits for them, and re-layouts, shards(): weighted[source]  15.9 us
    unnamed x1, blocking collectives  15 us
    gather x1, local copies, waits for them, and re-layouts, shards(): back_flat[slot_index].astype(jnp.float32)  14.4 us
  transfers between devices with their start and end apart: 2, of which 2 were waited for; matrix products, arithmetic and copies ran while one was open for 6% of the time, Pallas kernels for 0%

commit v1 on v0

v1 whole, which is shorter than its diff:
```python
import functools

import jax
import jax.numpy as jnp
from jax import lax
from jax.experimental import pallas as pl
from jax.experimental.pallas import tpu as pltpu
from jax.sharding import PartitionSpec as P

TOP = 10


EPSILON = 1e-06


def flipped(index, bit):
    return index + (1 - 2 * ((index // (1 << bit)) % 2)) * (1 << bit)


def spread_kernel(dp_count, seq_count, count, orders, total_sends, *refs):
    ins, outs = refs[:count], refs[count : 2 * count]
    holds = refs[2 * count : 3 * count]
    send_sem, recv_sem, local_sem = refs[3 * count :]
    devices = dp_count * seq_count
    dp, z = lax.axis_index("dp"), lax.axis_index("seq")
    own = dp * seq_count + z
    pending = []

    def guarded(conds, action):
        if not conds:
            action()
            return
        whole = conds[0]
        for extra in conds[1:]:
            whole = jnp.logical_and(whole, extra)
        pl.when(whole)(action)

    def send(array, source, block, target_dp, target_z, conds):
        copy = pltpu.make_async_remote_copy(
            src_ref=source,
            dst_ref=outs[array].at[block],
            send_sem=send_sem.at[len(pending)],
            recv_sem=recv_sem.at[array * devices + block],
            device_id=(target_dp, target_z),
            device_id_type=pl.DeviceIdType.MESH,
        )
        guarded(conds, copy.start)
        pending.append((conds, copy))

    def fan_out(array, first, source, block, conds):
        for bit in orders[array][first:]:
            send(array, source, block, flipped(dp, bit), z, conds)

    def arrived(array, block, conds):
        copy = pltpu.make_async_remote_copy(
            src_ref=outs[array].at[block],
            dst_ref=outs[array].at[block],
            send_sem=send_sem.at[0],
            recv_sem=recv_sem.at[array * devices + block],
            device_id=(flipped(dp, 0), z),
            device_id_type=pl.DeviceIdType.MESH,
        )
        guarded(conds, copy.wait_recv)

    taken = [
        pltpu.make_async_copy(ins[a], holds[a], local_sem.at[2 * a]) for a in range(count)
    ]
    put = [
        pltpu.make_async_copy(holds[a], outs[a].at[own], local_sem.at[2 * a + 1])
        for a in range(count)
    ]
    for copy in taken:
        copy.start()
    for array in range(count):
        send(array, ins[array], own, dp, z + 1, [z + 1 < seq_count])
        send(array, ins[array], own, dp, z - 1, [z > 0])
        fan_out(array, 0, ins[array], own, [])
    for a in range(count):
        taken[a].wait()
        put[a].start()

    def line_round(step):
        for array in range(count):
            for way in (1, -1):
                origin = z - way * step
                there = [origin >= 0, origin < seq_count]
                block = dp * seq_count + origin
                arrived(array, block, there)
                source = outs[array].at[block]
                if step < seq_count - 1:
                    beyond = z + way
                    onward = there + [beyond >= 0, beyond < seq_count]
                    send(array, source, block, dp, beyond, onward)
                fan_out(array, 0, source, block, there)

    def bit_round(stage, step):
        for array in range(count):
            order = orders[array]
            for combo in range(1 << stage):
                origin_dp = flipped(dp, order[stage])
                for place in range(stage):
                    if (combo >> place) & 1:
                        origin_dp = flipped(origin_dp, order[place])
                for offset in (0,) if step == 0 else (-step, step):
                    origin = z + offset
                    there = [] if step == 0 else [origin >= 0, origin < seq_count]
                    block = origin_dp * seq_count + origin
                    arrived(array, block, there)
                    fan_out(array, stage + 1, outs[array].at[block], block, there)

    for step in range(1, seq_count):
        line_round(step)
        bit_round(0, step - 1)
    bit_round(0, seq_count - 1)
    for stage in range(1, len(orders[0])):
        for step in range(seq_count):
            bit_round(stage, step)
    for copy in put:
        copy.wait()
    for conds, copy in pending:
        guarded(conds, copy.wait_send)
    assert len(pending) == total_sends


def spread(arrays, dp_count, seq_count):
    count = len(arrays)
    devices = dp_count * seq_count
    bits = (dp_count - 1).bit_length()
    upward = tuple(range(1, bits)) + (0,)
    downward = tuple(range(bits - 1, 0, -1)) + (0,)
    orders = [downward if a % 2 else upward for a in range(count)]
    calls = 2 * seq_count - 1
    per_array = 2 * (seq_count - 1) + calls * ((1 << bits) - 1)
    anywhere = pl.BlockSpec(memory_space=pl.ANY)
    return pl.pallas_call(
        functools.partial(
            spread_kernel, dp_count, seq_count, count, orders, count * per_array
        ),
        out_shape=[jax.ShapeDtypeStruct((devices,) + a.shape, a.dtype) for a in arrays],
        in_specs=[anywhere] * count,
        out_specs=[anywhere] * count,
        scratch_shapes=[pltpu.VMEM(a.shape, a.dtype) for a in arrays]
        + [
            pltpu.SemaphoreType.DMA((count * per_array,)),
            pltpu.SemaphoreType.DMA((count * devices,)),
            pltpu.SemaphoreType.DMA((2 * count,)),
        ],
        compiler_params=pltpu.CompilerParams(
            has_side_effects=True, vmem_limit_bytes=16 * 1024 * 1024
        ),
        cost_estimate=pl.CostEstimate(flops=0, bytes_accessed=200_000_000, transcendentals=0),
    )(*arrays)


def shards(
    hidden_in, cotangent, norm_gain, route_weights, expert_ids, expert_gate, expert_up, expert_down
):
    tokens_here = hidden_in.shape[1]
    model_width = hidden_in.shape[2]
    local_experts = expert_gate.shape[0]
    dp_count = lax.axis_size("dp")
    seq_count = lax.axis_size("seq")
    devices = dp_count * seq_count
    expert_count = local_experts * devices
    capacity = max(2, tokens_here * TOP * 6 // (5 * expert_count))
    own_weights = route_weights[0].T
    own_ids = expert_ids[0].T
    gain_rows = norm_gain.shape[0] // tokens_here
    table = jnp.concatenate(
        [own_weights, own_ids.astype(jnp.float32), norm_gain.reshape(gain_rows, tokens_here)],
        axis=0,
    )
    table = jnp.pad(table, ((0, -table.shape[0] % 8), (0, 0)))
    all_tables, all_hidden, all_upstream = spread(
        (table, hidden_in[0], cotangent[0]), dp_count, seq_count
    )
    gain_full = all_tables.reshape(dp_count, seq_count, -1, tokens_here)[
        :, 0, 2 * TOP : 2 * TOP + gain_rows
    ].reshape(model_width)
    position = jnp.arange(tokens_here, dtype=jnp.int32)
    earlier = (position[:, None] < position[None, :]).astype(jnp.bfloat16)
    slots = jnp.arange(capacity, dtype=jnp.int32).astype(jnp.float32)

    my_device = lax.axis_index("dp") * seq_count + lax.axis_index("seq")
    mine = (my_device * local_experts + jnp.arange(local_experts, dtype=jnp.int32)).astype(
        jnp.float32
    )
    matches = all_tables[:, None, TOP : 2 * TOP, :] == mine[None, :, None, None]
    named = jnp.any(matches, axis=2)
    token_weight = jnp.sum(jnp.where(matches, all_tables[:, None, :TOP, :], 0.0), axis=2)
    before = jnp.einsum(
        "nit,tu->niu", named.astype(jnp.bfloat16), earlier, preferred_element_type=jnp.float32
    )
    chosen = named[:, :, None, :] & (before[:, :, None, :] == slots[None, None, :, None])
    pick = chosen.astype(jnp.bfloat16)
    row_weight = jnp.sum(jnp.where(chosen, token_weight[:, :, None, :], 0.0), axis=3)
    pick_flat = pick.reshape(devices, local_experts * capacity, tokens_here)
    four_shape = (devices, local_experts, capacity, model_width)

    picked = jnp.einsum(
        "nst,ntd->nsd", pick_flat, all_hidden, preferred_element_type=jnp.float32
    ).astype(jnp.bfloat16)
    picked32 = picked.astype(jnp.float32)
    picked_root = lax.rsqrt(jnp.mean(picked32 * picked32, axis=2, keepdims=True) + EPSILON)
    rows_in = (
        (picked32 * picked_root * gain_full[None, None, :])
        .astype(jnp.bfloat16)
        .reshape(four_shape)
    )
    rows_grad = (
        jnp.einsum("nst,ntd->nsd", pick_flat, all_upstream, preferred_element_type=jnp.float32)
        * row_weight.reshape(devices, local_experts * capacity)[:, :, None]
    ).astype(jnp.bfloat16).reshape(four_shape)

    pre_gate = jnp.einsum(
        "nicd,idf->nicf", rows_in, expert_gate, preferred_element_type=jnp.float32
    )
    pre_up = jnp.einsum("nicd,idf->nicf", rows_in, expert_up, preferred_element_type=jnp.float32)
    sigmoid_gate = jax.nn.sigmoid(pre_gate)
    silu_gate = pre_gate * sigmoid_gate
    activation = (silu_gate * pre_up).astype(jnp.bfloat16)
    grad_act = jnp.einsum(
        "nicd,ifd->nicf", rows_grad, expert_down, preferred_element_type=jnp.float32
    )
    gate_back = (grad_act * pre_up * sigmoid_gate * (1.0 + pre_gate * (1.0 - sigmoid_gate))).astype(
        jnp.bfloat16
    )
    up_back = (grad_act * silu_gate).astype(jnp.bfloat16)
    grad_down = jnp.einsum(
        "nicf,nicd->ifd", activation, rows_grad, preferred_element_type=jnp.float32
    ).astype(jnp.bfloat16)
    grad_gate = jnp.einsum(
        "nicd,nicf->idf", rows_in, gate_back, preferred_element_type=jnp.float32
    ).astype(jnp.bfloat16)
    grad_up = jnp.einsum(
        "nicd,nicf->idf", rows_in, up_back, preferred_element_type=jnp.float32
    ).astype(jnp.bfloat16)
    returned = (
        jnp.einsum("nicf,idf->nicd", gate_back, expert_gate, preferred_element_type=jnp.float32)
        + jnp.einsum("nicf,idf->nicd", up_back, expert_up, preferred_element_type=jnp.float32)
    ).astype(jnp.bfloat16)
    back_rows = lax.all_to_all(
        returned.reshape(devices, local_experts * capacity, model_width),
        ("dp", "seq"),
        split_axis=0,
        concat_axis=0,
        tiled=True,
    )
    back_flat = back_rows.reshape(expert_count * capacity, model_width)

    every = jnp.arange(expert_count, dtype=jnp.int32)
    own_named = jnp.any(own_ids[None, :, :] == every[:, None, None], axis=1)
    own_before = jnp.dot(
        own_named.astype(jnp.bfloat16), earlier, preferred_element_type=jnp.float32
    )
    own_pick = (
        (own_named[:, None, :] & (own_before[:, None, :] == slots[None, :, None]))
        .astype(jnp.bfloat16)
        .reshape(expert_count * capacity, tokens_here)
    )
    summed = jnp.einsum("st,sd->td", own_pick, back_flat, preferred_element_type=jnp.float32)

    inputs = hidden_in[0].astype(jnp.float32)
    upstream = cotangent[0]
    inverse_root = lax.rsqrt(jnp.mean(inputs * inputs, axis=1, keepdims=True) + EPSILON)
    scaled = inputs * inverse_root
    local_gain = jnp.sum(summed * scaled, axis=0)
    partial_share = lax.psum_scatter(local_gain, "dp", scatter_dimension=0, tiled=True)
    grad_gain = lax.psum(partial_share, "seq")
    gained = summed * gain_full[None, :]
    centered = jnp.mean(gained * scaled, axis=1, keepdims=True)
    grad_hidden = (
        upstream.astype(jnp.float32) + inverse_root * (gained - scaled * centered)
    ).astype(jnp.bfloat16)
    return (grad_hidden.reshape(hidden_in.shape), grad_gain, grad_gate, grad_up, grad_down)


def solution(mesh):
    return jax.shard_map(
        shards,
        mesh=mesh,
        in_specs=(
            P("dp", "seq", None),
            P("dp", "seq", None),
            P("dp"),
            P("dp", "seq", None),
            P("dp", "seq", None),
            P(("dp", "seq"), None, None),
            P(("dp", "seq"), None, None),
            P(("dp", "seq"), None, None),
        ),
        out_specs=(
            P("dp", "seq", None),
            P("dp"),
            P(("dp", "seq"), None, None),
            P(("dp", "seq"), None, None),
            P(("dp", "seq"), None, None),
        ),
        check_vma=False,
    )
```

time: 606 us -> 406 us (0.67); the launches traced: 599 us -> 406 us
  blocking collectives: 179 us -> 26.1 us
  Pallas kernels: 0 us -> 151 us
  waiting for transfers between devices: 236 us -> 108 us
  local copies, waits for them, and re-layouts: 80.5 us -> 18.6 us
  matrix products: 62 us -> 89.5 us
  other arithmetic: 28 us -> 5.4 us
  starting transfers between devices: 11.9 us -> 5.15 us
    pallas_call x0 -> x1, Pallas kernels: none -> 151 us  [spread(): pl.pallas_call(functools.partial(spread_kernel, dp_count, seq_count, coun...]
    all_to_all x1 -> x0, blocking collectives: 142 us -> none  [shards(): lax.all_to_all(send_rows, ('dp', 'seq'), split_axis=0, concat_axis=0, til...]
    all_to_all x2 -> x1, waiting for transfers between devices: 236 us -> 108 us  [shards(): lax.all_to_all(returned.reshape(devices, local_experts * capacity, model_...]
    gather x3 -> x0, local copies, waits for them, and re-layouts: 37.4 us -> none  [the longest x1 15.9 us: shards(): weighted[source]]
    mul x5 -> x1, local copies, waits for them, and re-layouts: 22.2 us -> 0.07 us  [shards(): jnp.einsum('nst,ntd->nsd', pick_flat, all_upstream, preferred_element_typ...]
    dot_general x1 -> x5, matrix products: 0.82 us -> 20.9 us  [the longest x1 8.27 us: shards(): jnp.einsum('nst,ntd->nsd', pick_flat, all_upstream, preferred_element_typ...]
    unnamed x48 -> x37, local copies, waits for them, and re-layouts: 1.68 us -> 14.9 us
    convert_element_type x1 -> x0, local copies, waits for them, and re-layouts: 10.6 us -> none  [shards(): back_flat[slot_index].astype(jnp.float32)]
  transfers between devices with their start and end apart: 2 -> 1, of which waited for: 2 -> 1; matrix products, arithmetic and copies ran while one was open for 6% -> 7% of each run, Pallas kernels for 0% -> 0%
where the time goes in v1:
time: 406 us
  Pallas kernels  151 us (37%)
  waiting for transfers between devices  108 us (27%)
  matrix products  89.5 us (22%)
  blocking collectives  26.1 us (6%)
  local copies, waits for them, and re-layouts  18.6 us (5%)
  other arithmetic  5.4 us (1%)
  starting transfers between devices  5.15 us (1%)
    pallas_call x1, Pallas kernels, spread(): pl.pallas_call(functools.partial(spread_kernel, dp_count, seq_count, coun...  151 us
    all_to_all x1, waiting for transfers between devices, shards(): lax.all_to_all(returned.reshape(devices, local_experts * capacity, model_...  108 us
    unnamed x1, blocking collectives  15 us
    unnamed x37, local copies, waits for them, and re-layouts  14.9 us
    psum x1, blocking collectives, shards(): grad_gain = lax.psum(partial_share, 'seq')  11.1 us
    dot_general x1, matrix products, shards(): jnp.einsum('nicd,ifd->nicf', rows_grad, expert_down, preferred_element_ty...  9.95 us
    dot_general x1, matrix products, shards(): jnp.einsum('nicf,idf->nicd', gate_back, expert_gate, preferred_element_ty...  9.85 us
    dot_general x1, matrix products, shards(): jnp.einsum('nicd,idf->nicf', rows_in, expert_gate, preferred_element_type...  9.6 us
  transfers between devices with their start and end apart: 1, of which 1 were waited for; matrix products, arithmetic and copies ran while one was open for 7% of the time, Pallas kernels for 0%

profile of v1, /device:TPU:0, one launch (start us, length us, event | category | flops | bytes accessed | tf_op | source)
XLA Modules:
  0.0 405.9 jit_solution(8086246350920235292)
XLA Ops:
  0.7 0.7 copy.88
  1.4 0.7 fusion.50
  2.0 0.7 select_maximum_fusion.refs_0_
  2.7 1.0 copy-done.2
  3.8 1.0 copy-done.4
  4.8 151.4 %shard_map.119 = (f32[32,24,128]{2,1,0:T(8,128)S(1)}, bf16[32,128,2048]{2,1,0:T(8,128)(2,1)S(1)}, bf16[32,128,2048]{2,1,0:T(8,128)(2,1)S(1)}) custom-call(f32[24,128]{1,0:T(8,128)S(1)} %select_maximum_fusion.refs_0_, bf16[128,2048]{1,0:T(8,128)(2,1)S(1)} %bitcast.121, bf16[128,2048]{1,0:T(8,128)(2,1)S(1)} %bitcast.122), custom_call_target="tpu_custom_call" | custom-call | bytes 200000000 | tf_op jit(solution)/shard_map/pallas_call | solution.py:135
  156.2 5.7 %copy-done = bf16[32,128,2048]{2,1,0:T(8,128)(2,1)} copy-done((bf16[32,128,2048]{2,1,0:T(8,128)(2,1)}, bf16[32,128,2048]{2,1,0:T(8,128)(2,1)S(1)}, u32[]{:S(2)}) %copy-start) | copy-done | bytes 16777240
  161.9 5.7 %copy-done.1 = bf16[32,128,2048]{2,1,0:T(8,128)(2,1)} copy-done((bf16[32,128,2048]{2,1,0:T(8,128)(2,1)}, bf16[32,128,2048]{2,1,0:T(8,128)(2,1)S(1)}, u32[]{:S(2)}) %copy-start.1) | copy-done | bytes 16777240
  167.6 0.1 copy.48
  167.7 0.1 compare_reduce_fusion
  167.9 0.1 fusion.48
  168.0 0.1 eq.83
  168.1 0.0 copy-start.12
  168.1 0.1 copy.51
  168.2 0.1 fusion.44
  168.3 0.4 select_reduce_fusion
  168.8 0.1 copy.53
  168.8 0.1 copy.54
  168.9 0.2 fusion.42
  169.1 8.2 %fusion = (f32[32,48]{1,0:T(8,128)S(1)}, bf16[32,48,2048]{2,1,0:T(8,128)(2,1)S(1)}) fusion(pred[32,48,128]{2,1,0:T(8,128)(4,1)S(1)} %fusion.42, bf16[32,128,2048]{2,1,0:T(8,128)(2,1)} %copy-done.1), kind=kOutput, calls=%fused_computation.2 | convolution fusion | flops 817887744 | bytes 23271424 | tf_op jit(solution)/shard_map/nst,ntd->nsd/dot_general | solution.py:200
  177.4 1.5 fusion.2
  178.9 0.0 copy-start.8
  178.9 9.6 %fusion.4 = f32[2,32,24,512]{3,2,1,0:T(8,128)} fusion(bf16[32,2,24,2048]{3,2,1,0:T(8,128)(2,1)S(1)} %bitcast.127, bf16[2,2048,512]{2,1,0:T(8,128)(2,1)} %param.13), kind=kOutput, calls=%fused_computation.11 | convolution fusion | flops 3221225472 | bytes 13631488 | tf_op jit(solution)/shard_map/nicd,idf->nicf/dot_general | solution.py:215
  188.5 5.1 %fusion.6 = f32[2,32,24,512]{3,2,1,0:T(8,128)} fusion(bf16[32,2,24,2048]{3,2,1,0:T(8,128)(2,1)S(1)} %bitcast.128, bf16[2,2048,512]{2,1,0:T(8,128)(2,1)S(1)} %copy-done.8), kind=kOutput, calls=%fused_computation.13 | convolution fusion | flops 3221225472 | bytes 13631488 | tf_op jit(solution)/shard_map/nicd,idf->nicf/dot_general | solution.py:218
  193.6 8.3 %multiply_convert_fusion = bf16[32,48,2048]{2,1,0:T(8,128)(2,1)S(1)} fusion(f32[32,48]{1,0:T(8,128)S(1)} %copy.54, pred[32,48,128]{2,1,0:T(8,128)(4,1)S(1)} %fusion.42, bf16[32,128,2048]{2,1,0:T(8,128)(2,1)} %copy-done), kind=kOutput, calls=%fused_computation.6 | convolution fusion | flops 811597824 | bytes 23271424 | tf_op jit(solution)/shard_map/nst,ntd->nsd/dot_general | solution.py:211
  201.9 9.9 %fusion.28 = (bf16[32,2,24,512]{3,2,0,1:T(8,128)(2,1)S(1)}, bf16[32,2,24,512]{3,2,0,1:T(8,128)(2,1)S(1)}) fusion(f32[2,32,24,512]{3,2,1,0:T(8,128)} %fusion.4, f32[2,32,24,512]{3,2,1,0:T(8,128)} %fusion.6, bf16[2,512,2048]{2,1,0:T(8,128)(2,1)} %param.15, bf16[32,2,24,2048]{3,2,1,0:T(8,128)(2,1)S(1)} %bitcast.125), kind=kOutput, calls=%fused_computation.40 | convolution fusion | flops 3231449088 | bytes 19922944 | tf_op jit(solution)/shard_map/nicd,ifd->nicf/dot_general | solution.py:222
  211.9 0.0 copy-start.9
  211.9 9.8 %fusion.12 = f32[2,32,24,2048]{3,2,1,0:T(8,128)} fusion(bf16[32,2,24,512]{3,2,0,1:T(8,128)(2,1)S(1)} %get-tuple-element.14, bf16[2,2048,512]{2,1,0:T(8,128)(2,1)} %param.13), kind=kOutput, calls=%fused_computation.20 | convolution fusion | flops 3221225472 | bytes 18350080 | tf_op jit(solution)/shard_map/nicf,idf->nicd/dot_general | solution.py:239
  221.7 7.7 %fusion.3 = bf16[32,2,24,2048]{3,2,0,1:T(8,128)(2,1)S(1)} fusion(f32[2,32,24,2048]{3,2,1,0:T(8,128)} %fusion.12, bf16[32,2,24,512]{3,2,0,1:T(8,128)(2,1)S(1)} %get-tuple-element.13, bf16[2,2048,512]{2,1,0:T(8,128)(2,1)} %param.14), kind=kOutput, calls=%fused_computation.10 | convolution fusion | flops 3227516928 | bytes 24641536 | tf_op jit(solution)/shard_map/nicf,idf->nicd/dot_general | solution.py:240
  229.5 3.2 copy.58
  232.7 5.1 %all-to-all-start = ((bf16[32,48,2048]{2,1,0:T(8,128)(2,1)}), bf16[32,48,2048]{2,1,0:T(8,128)(2,1)}, u32[]{:S(2)}, u32[]{:S(2)}) async-start(bf16[32,48,2048]{2,1,0:T(8,128)(2,1)} %bitcast.124), calls=%async_computation | async-start | bytes 12582912 | tf_op jit(solution)/shard_map/all_to_all | solution.py:242
  237.9 0.6 dynamic-slice
  239.2 0.0 copy-done.3
  239.2 0.2 fusion.41
  239.4 0.1 fusion.47
  239.5 0.2 compare_and_fusion
  239.8 0.0 copy-start.10
  239.8 8.8 %bitcast_convert_fusion.1 = bf16[2,2048,512]{2,1,0:T(8,128)(2,1)} fusion(bf16[32,2,24,2048]{3,2,1,0:T(8,128)(2,1)} %bitcast.129, bf16[32,2,24,512]{3,2,0,1:T(8,128)(2,1)} %copy-done.11), kind=kOutput, calls=%fused_computation.8 | convolution fusion | flops 3223322624 | bytes 12058624 | tf_op jit(solution)/shard_map/nicd,nicf->idf/dot_general | solution.py:235
  248.6 9.4 %bitcast_convert_fusion.2 = bf16[2,2048,512]{2,1,0:T(8,128)(2,1)} fusion(bf16[32,2,24,2048]{3,2,1,0:T(8,128)(2,1)} %bitcast.130, bf16[32,2,24,512]{3,2,0,1:T(8,128)(2,1)S(1)} %copy-done.10), kind=kOutput, calls=%fused_computation.9 | convolution fusion | flops 3223322624 | bytes 12058624 | tf_op jit(solution)/shard_map/nicd,nicf->idf/dot_general | solution.py:232
  258.0 0.0 copy-done.16
  258.0 8.1 %bitcast_convert_fusion = bf16[2,512,2048]{2,1,0:T(8,128)(2,1)} fusion(bf16[32,2,24,2048]{3,2,1,0:T(8,128)(2,1)} %bitcast.126, f32[2,32,24,512]{3,2,1,0:T(8,128)S(1)} %copy-done.16, f32[2,32,24,512]{3,2,1,0:T(8,128)S(1)} %copy-done.15), kind=kOutput, calls=%fused_computation.7 | convolution fusion | flops 3228041216 | bytes 16777216 | tf_op jit(solution)/shard_map/nicf,nicd->ifd/dot_general | solution.py:229
  266.2 108.2 %all-to-all-done = bf16[32,48,2048]{2,1,0:T(8,128)(2,1)} async-done(((bf16[32,48,2048]{2,1,0:T(8,128)(2,1)}), bf16[32,48,2048]{2,1,0:T(8,128)(2,1)}, u32[]{:S(2)}, u32[]{:S(2)}) %all-to-all-start) | async-done | bytes 6291488 | tf_op jit(solution)/shard_map/all_to_all | solution.py:242
  374.4 4.1 %fusion.40 = (f32[2048]{0:T(1024)S(1)}, f32[128]{0:T(128)S(1)}, f32[128,2048]{1,0:T(8,128)S(1)}) fusion(f32[128]{0:T(128)S(1)} %add_rsqrt_fusion.1, bf16[1,128,2048]{2,1,0:T(8,128)(2,1)S(1)} %copy-done.3, f32[2048]{0:T(1024)S(1)} %bitcast.133, pred[1536,128]{1,0:T(8,128)(4,1)S(1)} %bitcast.131, bf16[1536,2048]{1,0:T(8,128)(2,1)} %bitcast.26), kind=kOutput, calls=%fused_computation.53 | convolution fusion | flops 807139200 | bytes 8078336 | tf_op jit(solution)/shard_map/st,sd->td/dot_general | solution.py:261
  378.5 15.0 %all-reduce.1 = f32[2048]{0:T(1024)S(1)} all-reduce(f32[2048]{0:T(1024)S(1)} %get-tuple-element.11), channel_id=2, replica_groups=mesh['dp'=8,'seq'=4] {'dp'}, use_global_device_ids=true, to_apply=%region_8.9.clone | all-reduce | flops 2048 | bytes 16384
  393.5 0.1 dynamic-slice.1
  393.6 11.1 %psum.7 = f32[256]{0:T(256)} all-reduce(f32[256]{0:T(256)S(1)} %dynamic-slice.1), channel_id=1, replica_groups=mesh['dp'=8,'seq'=4] {'seq'}, use_global_device_ids=true, to_apply=%region_9.10 | all-reduce | flops 256 | bytes 2048 | tf_op jit(solution)/shard_map/psum | solution.py:269
  404.7 0.0 copy-done.5
  404.7 1.2 fusion.43
  (35 shorter events, 0.2 us)
Async XLA Ops:
  2.7 1.0 copy-start.2
  3.8 1.0 copy-start.4
  156.2 5.7 %copy-start = (bf16[32,128,2048]{2,1,0:T(8,128)(2,1)}, bf16[32,128,2048]{2,1,0:T(8,128)(2,1)S(1)}, u32[]{:S(2)}) copy-start(bf16[32,128,2048]{2,1,0:T(8,128)(2,1)S(1)} %get-tuple-element.9) | copy-start | bytes 50331652
  161.9 5.7 %copy-start.1 = (bf16[32,128,2048]{2,1,0:T(8,128)(2,1)}, bf16[32,128,2048]{2,1,0:T(8,128)(2,1)S(1)}, u32[]{:S(2)}) copy-start(bf16[32,128,2048]{2,1,0:T(8,128)(2,1)S(1)} %get-tuple-element.10) | copy-start | bytes 50331652
  168.1 9.3 %copy-start.12 = (f32[8,1,2,128]{3,2,1,0:T(2,128)}, f32[8,1,2,128]{3,2,1,0:T(2,128)S(1)}, u32[]{:S(2)}) copy-start(f32[8,1,2,128]{3,2,1,0:T(2,128)S(1)} %slice.12) | copy-start | bytes 24580
  178.9 9.6 %copy-start.7 = (bf16[32,48,2048]{2,1,0:T(8,128)(2,1)}, bf16[32,48,2048]{2,1,0:T(8,128)(2,1)S(1)}, u32[]{:S(2)}) copy-start(bf16[32,48,2048]{2,1,0:T(8,128)(2,1)S(1)} %fusion.2) | copy-start | bytes 18874372
  178.9 9.6 %copy-start.8 = (bf16[2,2048,512]{2,1,0:T(8,128)(2,1)S(1)}, bf16[2,2048,512]{2,1,0:T(8,128)(2,1)}, u32[]{:S(2)}) copy-start(bf16[2,2048,512]{2,1,0:T(8,128)(2,1)} %param.14) | copy-start | bytes 12582916
  201.9 10.0 %copy-start.6 = (bf16[32,48,2048]{2,1,0:T(8,128)(2,1)}, bf16[32,48,2048]{2,1,0:T(8,128)(2,1)S(1)}, u32[]{:S(2)}) copy-start(bf16[32,48,2048]{2,1,0:T(8,128)(2,1)S(1)} %multiply_convert_fusion) | copy-start | bytes 18874372
  211.9 9.9 %copy-start.9 = (bf16[32,2,24,512]{3,2,0,1:T(8,128)(2,1)}, bf16[32,2,24,512]{3,2,0,1:T(8,128)(2,1)S(1)}, u32[]{:S(2)}) copy-start(bf16[32,2,24,512]{3,2,0,1:T(8,128)(2,1)S(1)} %get-tuple-element.14) | copy-start | bytes 4718596
  211.9 9.9 %copy-start.11 = (bf16[32,2,24,512]{3,2,0,1:T(8,128)(2,1)}, bf16[32,2,24,512]{3,2,0,1:T(8,128)(2,1)S(1)}, u32[]{:S(2)}) copy-start(bf16[32,2,24,512]{3,2,0,1:T(8,128)(2,1)S(1)} %get-tuple-element.13) | copy-start | bytes 4718596
  232.7 5.2 %copy-start.14 = (u32[32]{0:T(128)S(1)}, u32[32]{0:T(128)}, u32[]{:S(2)}) copy-start(u32[32]{0:T(128)} %constant.41) | copy-start | bytes 388
  232.7 6.5 %copy-start.3 = (bf16[1,128,2048]{2,1,0:T(8,128)(2,1)S(1)}, bf16[1,128,2048]{2,1,0:T(8,128)(2,1)}, u32[]{:S(2)}) copy-start(bf16[1,128,2048]{2,1,0:T(8,128)(2,1)} %param.8) | copy-start | bytes 1572868
  232.7 141.7 %all-to-all-start = ((bf16[32,48,2048]{2,1,0:T(8,128)(2,1)}), bf16[32,48,2048]{2,1,0:T(8,128)(2,1)}, u32[]{:S(2)}, u32[]{:S(2)}) async-start(bf16[32,48,2048]{2,1,0:T(8,128)(2,1)} %bitcast.124), calls=%async_computation | async-start | bytes 12582912 | tf_op jit(solution)/shard_map/all_to_all | solution.py:242
  239.8 8.8 %copy-start.10 = (bf16[32,2,24,512]{3,2,0,1:T(8,128)(2,1)S(1)}, bf16[32,2,24,512]{3,2,0,1:T(8,128)(2,1)}, u32[]{:S(2)}) copy-start(bf16[32,2,24,512]{3,2,0,1:T(8,128)(2,1)} %copy-done.9) | copy-start | bytes 4718596
  248.6 9.4 %copy-start.15 = (f32[2,32,24,512]{3,2,1,0:T(8,128)S(1)}, f32[2,32,24,512]{3,2,1,0:T(8,128)}, u32[]{:S(2)}) copy-start(f32[2,32,24,512]{3,2,1,0:T(8,128)} %fusion.4) | copy-start | bytes 9437188
  248.6 9.4 %copy-start.16 = (f32[2,32,24,512]{3,2,1,0:T(8,128)S(1)}, f32[2,32,24,512]{3,2,1,0:T(8,128)}, u32[]{:S(2)}) copy-start(f32[2,32,24,512]{3,2,1,0:T(8,128)} %fusion.6) | copy-start | bytes 9437188
  258.0 116.4 %copy-start.13 = (f32[8,1,2,128]{3,2,1,0:T(2,128)S(1)}, f32[8,1,2,128]{3,2,1,0:T(2,128)}, u32[]{:S(2)}) copy-start(f32[8,1,2,128]{3,2,1,0:T(2,128)} %copy-done.12) | copy-start | bytes 24580
  374.4 30.3 %copy-start.5 = (bf16[1,128,2048]{2,1,0:T(8,128)(2,1)S(1)}, bf16[1,128,2048]{2,1,0:T(8,128)(2,1)}, u32[]{:S(2)}) copy-start(bf16[1,128,2048]{2,1,0:T(8,128)(2,1)} %param.9) | copy-start | bytes 1572868
